TPU v7x, 256 devices: a 2x2x32 block of a 4x8x32 slice. The times are simulated.
256 devices in a mesh: replica: 4 (over x, y), tp: 32 (over z), sub: 2 (over core).
Axes of the slice: x: 2, y: 2, z: 32, core: 2. Of those that a mesh axis runs over, the one named last changes fastest.
The devices are a block of a 4x8x32 slice.
Arguments:
- hidden_in: bfloat16 [16, 8192], P('replica'), parts along dimension 0, may hold values from -6 to 6
- norm_gain: float32 [32768], P('replica'), parts along dimension 0, may hold values from 0.1 to 1.9
- wqkv_old: bfloat16 [128, 2, 1280, 1024], P(('replica', 'tp'), 'sub'), parts along dimension 0, may hold values from -0.1875 to 0.1875
- wo: bfloat16 [32768, 8192], P(('replica', 'tp', 'sub')), parts along dimension 0, may hold values from -0.0625 to 0.0625
- key_cache: bfloat16 [16, 4096, 1024], P('replica', ('tp', 'sub')), parts along dimension 0, may hold values from -240 to 240
- value_cache: bfloat16 [16, 4096, 1024], P('replica', ('tp', 'sub')), parts along dimension 0, may hold values from -6 to 6
- lengths: int32 [16], P('replica'), parts along dimension 0, may hold values from 1 to 4096
- section_order: int32 [64], P('replica'), parts along dimension 0, may hold values from 0 to 15, each once
Outputs:
- mixed_out: bfloat16 [16, 8192], P('replica'), parts along dimension 0
- wqkv_new: bfloat16 [128, 2, 160, 8192], P(('replica', 'tp'), 'sub'), parts along dimension 0
There are 4 independent parts, one for each index of `replica`. A program takes and returns all parts, laid end to end along the dimension named above; each array names one. Nothing has to cross between parts.
Inputs may be any that keep to these rules, and one draw needn't show every extreme that they name: `section_order`: each input row block appears once. The new token's position is lengths[b].
All inputs are finite; a program needn't handle non-finite values.
Results may differ from a plain program's by a relative error of at most 0.0085.
The roundings to bfloat16 on the way count: a program that leaves them out, or rounds other values in their place, can miss the bound.
Values may be sent and summed in bfloat16 or wider, within the bound.
A program may use at most 64 MiB of HBM per device.

v0:
```python
import math

import jax
import jax.numpy as jnp
from jax import lax
from jax.sharding import PartitionSpec as P

HEADS = 64
KV_HEADS = 8
HEAD_DIM = 128
RANKS = 8
ROW_BLOCKS = 16


def passed_along(value, axis, steps):
    count = lax.axis_size(axis)
    pairs = [(source, (source + steps) % count) for source in range(count)]
    return lax.ppermute(value, axis, pairs)


def laid_out(parts, dim):
    dims = list(parts.shape[1:])
    dims[dim] *= parts.shape[0]
    return jnp.moveaxis(parts, 0, dim).reshape(dims)


def from_everyone(x, axis):
    peers = lax.axis_size(axis)
    return lax.all_to_all(jnp.broadcast_to(x[None], (peers, *x.shape)), axis, 0, 0, tiled=True)


def collect(x, axis, dim):
    return laid_out(from_everyone(x, axis), dim)


def side_by_side(arrays, axis, split_dim, concat_dim, along):
    columns = [a.reshape(*a.shape[:along], -1) for a in arrays]
    both = jnp.concatenate(columns, axis=along)
    result, at, outs = (
        lax.all_to_all(both, axis, split_axis=split_dim, concat_axis=concat_dim, tiled=True),
        0,
        [],
    )
    for a, column in zip(arrays, columns):
        slab = result[..., at : at + column.shape[along]]
        outs.append(slab.reshape(*slab.shape[:along], *a.shape[along:]))
        at += column.shape[along]
    return tuple(outs)


def gathered_total(x, axis):
    parts = lax.all_gather(x, axis)
    return parts.sum(axis=0)


def rotary(values, positions):
    half = values.shape[-1] // 2
    freqs = 500000.0 ** (-jnp.arange(half, dtype=jnp.float32) * 2.0 / values.shape[-1])
    angles = positions.astype(jnp.float32)[:, None] * freqs[None, :]
    cosine = jnp.cos(angles)[:, None, :]
    sine = jnp.sin(angles)[:, None, :]
    first_half = values[..., :half]
    second_half = values[..., half:]
    return jnp.concatenate(
        [first_half * cosine - second_half * sine, second_half * cosine + first_half * sine], -1
    )


def rms_normed(hidden_in, norm_gain):
    widened = hidden_in.astype(jnp.float32)
    factor = lax.rsqrt(jnp.mean(widened * widened, -1, keepdims=True) + 1e-05)
    return (widened, (widened * factor * norm_gain).astype(jnp.bfloat16))


def shards(hidden_in, norm_gain, wqkv_old, wo, key_cache, value_cache, lengths, section_order):
    tp_count = lax.axis_size("tp")
    section_count = tp_count // 4
    per_section = ROW_BLOCKS // section_count
    tp_index = lax.axis_index("tp")
    sub_index = lax.axis_index("sub")
    own_section = tp_index // 4
    device_rank = tp_index * 2 + sub_index
    cols_dev = wqkv_old.shape[2] // section_count
    rows_old = wqkv_old.shape[3]
    block_rows = rows_old // per_section
    old_block = wqkv_old[0, 0].reshape(section_count, cols_dev, rows_old)
    slot_ids = jnp.arange(section_count, dtype=jnp.int32)
    arrived = [lax.dynamic_index_in_dim(old_block, own_section, 0, keepdims=False)]
    for offset in range(1, section_count):
        outgoing = lax.dynamic_index_in_dim(
            old_block, (own_section + offset) % section_count, 0, keepdims=False
        )
        arrived.append(passed_along(outgoing, "tp", 4 * offset))
    received = jnp.stack(arrived, 0)
    sources = (own_section - slot_ids) % section_count
    block_ids = jnp.arange(ROW_BLOCKS, dtype=jnp.int32)
    local_source = (
        sources[:, None] * per_section + jnp.arange(per_section, dtype=jnp.int32)[None, :]
    ).reshape(ROW_BLOCKS)
    target_block = jnp.take(section_order, local_source, axis=0)
    placing = (target_block[None, :] == block_ids[:, None]).astype(jnp.bfloat16)
    received_blocks = jnp.transpose(
        received.reshape(section_count, cols_dev, per_section, block_rows), (0, 2, 1, 3)
    ).reshape(ROW_BLOCKS, cols_dev, block_rows)
    new_weight = jnp.einsum(
        "sa,acr->csr", placing, received_blocks, preferred_element_type=jnp.float32
    ).astype(jnp.bfloat16)
    new_weight = new_weight.reshape(cols_dev, ROW_BLOCKS * block_rows)
    widened, normed = rms_normed(hidden_in, norm_gain)
    projected = lax.dot_general(
        normed, new_weight, (((1,), (1,)), ((), ())), preferred_element_type=jnp.float32
    ).astype(jnp.bfloat16)
    gathered = collect(projected[:, None, :], ("tp", "sub"), 1)
    seq_count = hidden_in.shape[0]
    projected_all = jnp.transpose(
        gathered.reshape(seq_count, section_count, RANKS, cols_dev), (0, 2, 1, 3)
    ).reshape(seq_count, -1)
    q_width = HEADS * HEAD_DIM
    kv_width = KV_HEADS * HEAD_DIM
    groups = HEADS // KV_HEADS
    queries = rotary(
        projected_all[:, :q_width].astype(jnp.float32).reshape(seq_count, HEADS, HEAD_DIM), lengths
    ).astype(jnp.bfloat16)
    new_keys = rotary(
        projected_all[:, q_width : q_width + kv_width]
        .astype(jnp.float32)
        .reshape(seq_count, KV_HEADS, HEAD_DIM),
        lengths,
    ).astype(jnp.bfloat16)
    new_values = (
        projected_all[:, q_width + kv_width :]
        .astype(jnp.float32)
        .reshape(seq_count, KV_HEADS, HEAD_DIM)
    )
    pos_count = key_cache.shape[1]
    positions = device_rank * pos_count + jnp.arange(pos_count, dtype=jnp.int32)
    usable = (positions[None, :] < lengths[:, None])[:, None, None, :]
    inverse = 1.0 / math.sqrt(HEAD_DIM)
    grouped = queries.reshape(seq_count, KV_HEADS, groups, HEAD_DIM)
    keys_local = key_cache.reshape(seq_count, pos_count, KV_HEADS, HEAD_DIM)
    values_local = value_cache.reshape(seq_count, pos_count, KV_HEADS, HEAD_DIM).astype(jnp.float32)
    scores = (
        jnp.einsum("bkgd,bpkd->bkgp", grouped, keys_local, preferred_element_type=jnp.float32)
        * inverse
    )
    local_top = jnp.max(jnp.where(usable, scores, -1e30), -1)
    weights = jnp.exp(jnp.where(usable, scores - local_top[..., None], -1e30))
    local_sum = jnp.sum(weights, -1).reshape(seq_count, HEADS)
    local_mix = jnp.einsum("bkgp,bpkd->bkgd", weights, values_local).reshape(
        seq_count, HEADS, HEAD_DIM
    )
    local_top = local_top.reshape(seq_count, HEADS)
    heads_dev = wo.shape[0] // HEAD_DIM
    first_head = device_rank * heads_dev
    tops_in, sums_in, mixes_in = side_by_side(
        (local_top[None], local_sum[None], local_mix[None]), ("tp", "sub"), 2, 0, 3
    )
    best = jnp.max(tops_in, 0)
    factors = jnp.exp(tops_in - best[None])
    head_sum = jnp.sum(sums_in * factors, 0)
    head_mix = jnp.sum(mixes_in * factors[..., None], 0)
    own_queries = lax.dynamic_slice_in_dim(queries, first_head, heads_dev, 1).astype(jnp.float32)
    kv_index = (first_head + jnp.arange(heads_dev, dtype=jnp.int32)) // groups
    own_keys = jnp.take(new_keys, kv_index, axis=1).astype(jnp.float32)
    own_values = jnp.take(new_values, kv_index, axis=1)
    own_score = jnp.sum(own_queries * own_keys, -1) * inverse
    highest = jnp.maximum(best, own_score)
    old_scale = jnp.exp(best - highest)
    own_weight = jnp.exp(own_score - highest)
    numerator = head_mix * old_scale[..., None] + own_weight[..., None] * own_values
    denominator = head_sum * old_scale + own_weight
    attended = (
        (numerator / denominator[..., None])
        .reshape(seq_count, heads_dev * HEAD_DIM)
        .astype(jnp.bfloat16)
    )
    partial_out = jnp.dot(attended, wo, preferred_element_type=jnp.float32)
    summed_out = gathered_total(partial_out, ("tp", "sub"))
    mixed_out = (widened + summed_out).astype(jnp.bfloat16)
    return (mixed_out, new_weight[None, None])


def solution(mesh):
    placed = (
        P("replica", None),
        P("replica"),
        P(("replica", "tp"), "sub", None, None),
        P(("replica", "tp", "sub"), None),
        P("replica", ("tp", "sub"), None),
        P("replica", ("tp", "sub"), None),
        P("replica"),
        P("replica"),
    )
    return jax.shard_map(
        shards,
        mesh=mesh,
        in_specs=placed,
        out_specs=(P("replica", None), P(("replica", "tp"), "sub", None, None)),
        check_vma=False,
    )
```

profile of v0, /device:TPU:103, one launch (start us, length us, event | category | flops | bytes accessed | tf_op | source)
XLA Modules:
  0.0 529.6 jit_solution(14706307084161187386)
XLA Ops:
  7.4 3.0 dynamic-slice_bitcast_fusion
  10.4 22.6 %collective-permute-start.6 = (bf16[160,1024]{1,0:T(8,128)(2,1)S(1)}, bf16[160,1024]{1,0:T(8,128)(2,1)}, u32[]{:S(2)}, u32[]{:S(2)}) collective-permute-start(bf16[160,1024]{1,0:T(8,128)(2,1)S(1)} %get-tuple-element.29), channel_id=1, source_target_pairs={{0,56},{2,58},{4,60},{6,62},{8,0},{10,2},{12,4},{14,6},{16,8},{18,... | collective-permute-start | bytes 983048 | tf_op jit(solution)/shard_map/ppermute | solution.py:18
  33.0 4.6 collective-permute-start.5
  37.6 2.2 collective-permute-start.4
  39.8 10.2 %collective-permute-start.1 = (bf16[160,1024]{1,0:T(8,128)(2,1)}, bf16[160,1024]{1,0:T(8,128)(2,1)}, u32[]{:S(2)}, u32[]{:S(2)}) collective-permute-start(bf16[160,1024]{1,0:T(8,128)(2,1)} %get-tuple-element.34), channel_id=1, source_target_pairs={{0,16},{2,18},{4,20},{6,22},{8,24},{10,26},{12,28},{14,30},{16,32}... | collective-permute-start | bytes 983048 | tf_op jit(solution)/shard_map/ppermute | solution.py:18
  50.0 2.9 collective-permute-start
  53.2 0.7 gather_fusion
  53.8 0.2 fusion.10
  54.1 48.1 %collective-permute-done = bf16[160,1024]{1,0:T(8,128)(2,1)} collective-permute-done((bf16[160,1024]{1,0:T(8,128)(2,1)}, bf16[160,1024]{1,0:T(8,128)(2,1)}, u32[]{:S(2)}, u32[]{:S(2)}) %collective-permute-start) | collective-permute-done | bytes 327712 | tf_op jit(solution)/shard_map/ppermute | solution.py:18
  102.1 11.4 %collective-permute-start.2 = (bf16[160,1024]{1,0:T(8,128)(2,1)}, bf16[160,1024]{1,0:T(8,128)(2,1)S(1)}, u32[]{:S(2)}, u32[]{:S(2)}) collective-permute-start(bf16[160,1024]{1,0:T(8,128)(2,1)} %get-tuple-element.33), channel_id=1, source_target_pairs={{0,24},{2,26},{4,28},{6,30},{8,32},{10,34},{12,36},{14,38},{16,40}... | collective-permute-start | bytes 983048 | tf_op jit(solution)/shard_map/ppermute | solution.py:18
  113.5 1.7 bitcast_dynamic-update-slice_fusion.6
  115.2 3.4 collective-permute-start.3
  118.6 1.7 bitcast_dynamic-update-slice_fusion.5
  120.3 65.2 %collective-permute-done.2 = bf16[160,1024]{1,0:T(8,128)(2,1)S(1)} collective-permute-done((bf16[160,1024]{1,0:T(8,128)(2,1)}, bf16[160,1024]{1,0:T(8,128)(2,1)S(1)}, u32[]{:S(2)}, u32[]{:S(2)}) %collective-permute-start.2) | collective-permute-done | bytes 327712 | tf_op jit(solution)/shard_map/ppermute | solution.py:18
  185.5 0.7 bitcast_dynamic-update-slice_fusion.4
  186.2 69.7 %collective-permute-done.3 = bf16[160,1024]{1,0:T(8,128)(2,1)S(1)} collective-permute-done((bf16[160,1024]{1,0:T(8,128)(2,1)S(1)}, bf16[160,1024]{1,0:T(8,128)(2,1)S(1)}, u32[]{:S(2)}, u32[]{:S(2)}) %collective-permute-start.3) | collective-permute-done | bytes 327712 | tf_op jit(solution)/shard_map/ppermute | solution.py:18
  255.9 0.7 bitcast_dynamic-update-slice_fusion.3
  256.7 1.7 bitcast_dynamic-update-slice_fusion.2
  258.4 1.7 bitcast_dynamic-update-slice_fusion.1
  260.1 1.7 bitcast_dynamic-update-slice_fusion
  261.8 1.9 fusion.53
  263.8 0.2 pad_maximum_fusion
  263.9 1.7 fusion.2
  265.7 1.8 copy.67
  267.5 0.8 convolution_convert_fusion
  268.3 0.7 broadcast_in_dim.35
  269.1 43.2 %all-to-all-start = ((bf16[64,4,1,160]{3,1,2,0:T(4,128)(2,1)}), bf16[64,4,1,160]{3,1,2,0:T(4,128)(2,1)S(1)}, u32[]{:S(2)}, u32[]{:S(2)}) async-start(bf16[64,4,1,160]{3,1,2,0:T(4,128)(2,1)} %broadcast_in_dim.35), calls=%async_computation | async-start | bytes 262144 | tf_op jit(solution)/shard_map/all_to_all | solution.py:29
  312.5 28.9 %all-to-all-done = bf16[64,4,1,160]{3,1,2,0:T(4,128)(2,1)S(1)} async-done(((bf16[64,4,1,160]{3,1,2,0:T(4,128)(2,1)}), bf16[64,4,1,160]{3,1,2,0:T(4,128)(2,1)S(1)}, u32[]{:S(2)}, u32[]{:S(2)}) %all-to-all-start) | async-done | bytes 81952 | tf_op jit(solution)/shard_map/all_to_all | solution.py:29
  341.4 0.2 reshape.375
  341.8 0.5 select_reduce_fusion
  342.4 0.2 fusion.14
  342.6 1.3 convolution_bitcast_fusion.1
  344.2 0.1 copy.57
  344.3 0.1 copy.56
  344.5 1.0 pad_maximum_fusion.1
  345.5 7.5 %all-to-all-start.1 = ((f32[1,4,64,130]{3,1,0,2:T(4,128)}), f32[1,4,64,130]{3,1,0,2:T(4,128)S(1)}, u32[]{:S(2)}, u32[]{:S(2)}) async-start(f32[1,4,64,130]{3,1,0,2:T(4,128)} %pad_maximum_fusion.1), calls=%async_computation.1 | async-start | bytes 524288 | tf_op jit(solution)/shard_map/all_to_all | solution.py:40
  353.3 0.1 copy.64
  353.6 0.1 copy.63
  353.7 0.2 copy.62
  354.0 39.7 %all-to-all-done.1 = f32[1,4,64,130]{3,1,0,2:T(4,128)S(1)} async-done(((f32[1,4,64,130]{3,1,0,2:T(4,128)}), f32[1,4,64,130]{3,1,0,2:T(4,128)S(1)}, u32[]{:S(2)}, u32[]{:S(2)}) %all-to-all-start.1) | async-done | bytes 133152 | tf_op jit(solution)/shard_map/all_to_all | solution.py:40
  393.7 0.2 copy.59
  394.1 0.2 fusion.41
  394.3 0.2 fusion.9
  394.6 1.1 convolution_bitcast_fusion
  395.7 5.3 broadcast_in_dim_reshape.7
  401.0 116.3 %all-gather.4.cloned.1.call-done = f32[64,4,8192]{2,1,0:T(4,128)} async-done(((f32[1,4,8192]{2,1,0:T(4,128)}), f32[64,4,8192]{2,1,0:T(4,128)}) %all-gather.4.cloned.1.call-update) | async-done | bytes 8388624 | tf_op jit(solution)/shard_map/all_gather | solution.py:52
  517.3 4.8 reduce_sum.59
  522.1 0.7 fusion.13
  (50 shorter events, 1.6 us)
Async XLA Ops:
  7.2 387.4 %copy-start = (bf16[128,8192]{1,0:T(8,128)(2,1)S(1)}, bf16[128,8192]{1,0:T(8,128)(2,1)}, u32[]{:S(2)}) copy-start(bf16[128,8192]{1,0:T(8,128)(2,1)} %param.11) | copy-start | bytes 6291460
  7.4 45.8 %copy-start.1 = (s32[16]{0:T(128)S(1)}, s32[16]{0:T(128)}, u32[]{:S(2)}) copy-start(s32[16]{0:T(128)} %param.15) | copy-start | bytes 196
  7.4 46.5 %copy-start.3 = (bf16[4,8192]{1,0:T(4,128)(2,1)S(1)}, bf16[4,8192]{1,0:T(4,128)(2,1)}, u32[]{:S(2)}) copy-start(bf16[4,8192]{1,0:T(4,128)(2,1)} %param.8) | copy-start | bytes 196612
  7.4 46.7 %copy-start.6 = (s32[4]{0:T(128)S(1)}, s32[4]{0:T(128)}, u32[]{:S(2)}) copy-start(s32[4]{0:T(128)} %param.14) | copy-start | bytes 52
  10.4 249.7 %collective-permute-start.6 = (bf16[160,1024]{1,0:T(8,128)(2,1)S(1)}, bf16[160,1024]{1,0:T(8,128)(2,1)}, u32[]{:S(2)}, u32[]{:S(2)}) collective-permute-start(bf16[160,1024]{1,0:T(8,128)(2,1)S(1)} %get-tuple-element.29), channel_id=1, source_target_pairs={{0,56},{2,58},{4,60},{6,62},{8,0},{10,2},{12,4},{14,6},{16,8},{18,... | collective-permute-start | bytes 983048 | tf_op jit(solution)/shard_map/ppermute | solution.py:18
  33.0 225.4 %collective-permute-start.5 = (bf16[160,1024]{1,0:T(8,128)(2,1)S(1)}, bf16[160,1024]{1,0:T(8,128)(2,1)}, u32[]{:S(2)}, u32[]{:S(2)}) collective-permute-start(bf16[160,1024]{1,0:T(8,128)(2,1)S(1)} %get-tuple-element.30), channel_id=1, source_target_pairs={{0,48},{2,50},{4,52},{6,54},{8,56},{10,58},{12,60},{14,62},{16,0},... | collective-permute-start | bytes 983048 | tf_op jit(solution)/shard_map/ppermute | solution.py:18
  37.6 219.0 %collective-permute-start.4 = (bf16[160,1024]{1,0:T(8,128)(2,1)S(1)}, bf16[160,1024]{1,0:T(8,128)(2,1)}, u32[]{:S(2)}, u32[]{:S(2)}) collective-permute-start(bf16[160,1024]{1,0:T(8,128)(2,1)S(1)} %get-tuple-element.31), channel_id=1, source_target_pairs={{0,40},{2,42},{4,44},{6,46},{8,48},{10,50},{12,52},{14,54},{16,56}... | collective-permute-start | bytes 983048 | tf_op jit(solution)/shard_map/ppermute | solution.py:18
  39.8 75.5 %collective-permute-start.1 = (bf16[160,1024]{1,0:T(8,128)(2,1)}, bf16[160,1024]{1,0:T(8,128)(2,1)}, u32[]{:S(2)}, u32[]{:S(2)}) collective-permute-start(bf16[160,1024]{1,0:T(8,128)(2,1)} %get-tuple-element.34), channel_id=1, source_target_pairs={{0,16},{2,18},{4,20},{6,22},{8,24},{10,26},{12,28},{14,30},{16,32}... | collective-permute-start | bytes 983048 | tf_op jit(solution)/shard_map/ppermute | solution.py:18
  50.0 52.2 %collective-permute-start = (bf16[160,1024]{1,0:T(8,128)(2,1)}, bf16[160,1024]{1,0:T(8,128)(2,1)}, u32[]{:S(2)}, u32[]{:S(2)}) collective-permute-start(bf16[160,1024]{1,0:T(8,128)(2,1)} %get-tuple-element.35), channel_id=1, source_target_pairs={{0,8},{2,10},{4,12},{6,14},{8,16},{10,18},{12,20},{14,22},{16,24},... | collective-permute-start | bytes 983048 | tf_op jit(solution)/shard_map/ppermute | solution.py:18
  102.1 83.4 %collective-permute-start.2 = (bf16[160,1024]{1,0:T(8,128)(2,1)}, bf16[160,1024]{1,0:T(8,128)(2,1)S(1)}, u32[]{:S(2)}, u32[]{:S(2)}) collective-permute-start(bf16[160,1024]{1,0:T(8,128)(2,1)} %get-tuple-element.33), channel_id=1, source_target_pairs={{0,24},{2,26},{4,28},{6,30},{8,32},{10,34},{12,36},{14,38},{16,40}... | collective-permute-start | bytes 983048 | tf_op jit(solution)/shard_map/ppermute | solution.py:18
  115.2 140.7 %collective-permute-start.3 = (bf16[160,1024]{1,0:T(8,128)(2,1)S(1)}, bf16[160,1024]{1,0:T(8,128)(2,1)S(1)}, u32[]{:S(2)}, u32[]{:S(2)}) collective-permute-start(bf16[160,1024]{1,0:T(8,128)(2,1)S(1)} %get-tuple-element.32), channel_id=1, source_target_pairs={{0,32},{2,34},{4,36},{6,38},{8,40},{10,42},{12,44},{14,46},{16,48}... | collective-permute-start | bytes 983048 | tf_op jit(solution)/shard_map/ppermute | solution.py:18
  265.6 1.9 copy-start.2
  265.7 1.9 copy-start.5
  267.5 74.3 %copy-start.4 = (bf16[4,64,1024]{2,1,0:T(8,128)(2,1)S(1)}, bf16[4,64,1024]{2,1,0:T(8,128)(2,1)}, u32[]{:S(2)}) copy-start(bf16[4,64,1024]{2,1,0:T(8,128)(2,1)} %param.12) | copy-start | bytes 1572868
  269.1 72.3 %all-to-all-start = ((bf16[64,4,1,160]{3,1,2,0:T(4,128)(2,1)}), bf16[64,4,1,160]{3,1,2,0:T(4,128)(2,1)S(1)}, u32[]{:S(2)}, u32[]{:S(2)}) async-start(bf16[64,4,1,160]{3,1,2,0:T(4,128)(2,1)} %broadcast_in_dim.35), calls=%async_computation | async-start | bytes 262144 | tf_op jit(solution)/shard_map/all_to_all | solution.py:29
  345.5 48.2 %all-to-all-start.1 = ((f32[1,4,64,130]{3,1,0,2:T(4,128)}), f32[1,4,64,130]{3,1,0,2:T(4,128)S(1)}, u32[]{:S(2)}, u32[]{:S(2)}) async-start(f32[1,4,64,130]{3,1,0,2:T(4,128)} %pad_maximum_fusion.1), calls=%async_computation.1 | async-start | bytes 524288 | tf_op jit(solution)/shard_map/all_to_all | solution.py:40
  353.1 164.3 %all-gather.4.cloned.1.call-start = ((), (), s32[]{:S(2)}) async-start(), calls=%async_computation.2 | async-start | bytes 8519680 | tf_op jit(solution)/shard_map/all_gather | solution.py:52
Sparse Core Ops, SparseCore 0:
  395.9 121.4 all-gather.3
where the time goes:
time: 533 us; the launch traced here: 530 us
  waiting for transfers between devices  368 us (69%)
  starting transfers between devices  108 us (20%)
  local copies, waits for them, and re-layouts  25.2 us (5%)
  between operations  14.6 us (3%)
  other arithmetic  8.38 us (2%)
  matrix products  5.47 us (1%)
    ppermute x7, waiting for transfers between devices, passed_along(): return lax.ppermute(value, axis, pairs)  183 us
    all_gather x1, waiting for transfers between devices, gathered_total(): parts = lax.all_gather(x, axis)  116 us
    ppermute x7, starting transfers between devices, passed_along(): return lax.ppermute(value, axis, pairs)  57.3 us
    all_to_all x1, starting transfers between devices, from_everyone(): lax.all_to_all(jnp.broadcast_to(x[None], (peers, *x.shape)), axis, 0, 0,...  43.2 us
    all_to_all x1, waiting for transfers between devices, side_by_side(): lax.all_to_all(both, axis, split_axis=split_dim, concat_axis=concat_dim,...  39.7 us
    all_to_all x1, waiting for transfers between devices, from_everyone(): lax.all_to_all(jnp.broadcast_to(x[None], (peers, *x.shape)), axis, 0, 0,...  28.9 us
  transfers between devices with their start and end apart: 10, of which 6 were waited for; matrix products, arithmetic and copies ran while one was open for 3% of the time, Pallas kernels for 0%

commit v1 on v0

v1 whole, which is shorter than its diff:
```python
import functools
import math

import jax
import jax.numpy as jnp
from jax import lax
from jax.experimental import pallas as pl
from jax.experimental.pallas import tpu as pltpu
from jax.sharding import PartitionSpec as P

HEADS = 64
KV_HEADS = 8
HEAD_DIM = 128
ROW_BLOCKS = 16
NEAR = 4
SECTIONS = 8
STEP_ROWS = 8

MESH = pl.DeviceIdType.MESH
F32 = jnp.float32
BF16 = jnp.bfloat16


def nt_dot(x, y):
    return lax.dot_general(x, y, (((1,), (1,)), ((), ())), preferred_element_type=F32)


def split_stat(stat):
    low = lax.broadcasted_iota(jnp.int32, stat.shape, stat.ndim - 1) < 64
    turned = pltpu.roll(stat, 64, stat.ndim - 1)
    return jnp.where(low, stat, turned), jnp.where(low, turned, stat)


def merged(parts):
    best = parts[0][1]
    for _, top, _ in parts[1:]:
        best = jnp.maximum(best, top)
    mix, total = None, None
    for m, top, s in parts:
        f = jnp.exp(top - best)
        mix = m * f if mix is None else mix + m * f
        total = s * f if total is None else total + s * f
    return mix, best, total


def joined_stat(best, total):
    low = lax.broadcasted_iota(jnp.int32, best.shape, best.ndim - 1) < 64
    return jnp.where(low, best, total)


def main_kernel(
    hid, gain, turn, lengths, order, w, wo, kc, vc,
    recv, g_out,
    w_v, wo_v, k_v, v_v, nrm, p_tx, p_rx, q_tx, q_all, rows, state, a_rx1, a_rx2, a_tx, a_rx3,
    part, o_rx1, o_rx2, o_tx, o_rx3, g_all,
    load_sem, big_s, big_r, far_s, far_r, loc_s, loc_r, duo_s, duo_r, known_lo, known_hi,
):
    count = lax.axis_size("tp")
    t = lax.axis_index("tp")
    s = lax.axis_index("sub")
    a = t // NEAR
    c = t % NEAR
    seqs, width = hid.shape
    cols = recv.shape[1]

    def far_id(k):
        return {"tp": lax.rem(t + NEAR * k, count)}

    def loc_id(m):
        return {"tp": NEAR * a + lax.rem(c + m, NEAR)}

    duo_id = {"sub": 1 - s}

    barrier = pltpu.get_barrier_semaphore()
    greeted = [far_id(1), far_id(SECTIONS - 1), loc_id(1), loc_id(2), loc_id(3), duo_id]
    for target in greeted:
        pl.semaphore_signal(barrier, inc=1, device_id=target, device_id_type=MESH)

    loads = [
        pltpu.make_async_copy(src, dst, load_sem.at[i])
        for i, (src, dst) in enumerate(((w, w_v), (kc, k_v), (vc, v_v), (wo, wo_v)))
    ]
    loads[0].start()
    pl.semaphore_wait(barrier, len(greeted))

    sent = dict.fromkeys(range(1, SECTIONS), 0)

    def piece(k, row, height):
        b = lax.rem(a + k, SECTIONS)
        first = pl.multiple_of(b * cols + row, 8)
        return pltpu.make_async_remote_copy(
            src_ref=w.at[pl.ds(first, height), :],
            dst_ref=recv.at[a, pl.ds(row, height), :],
            send_sem=big_s.at[k],
            recv_sem=big_r.at[SECTIONS - k],
            device_id=far_id(k),
            device_id_type=MESH,
        )

    def stream(ks, n):
        ks = [k for k in ks if sent[k] < cols]
        n = min([n] + [(cols - sent[k]) // STEP_ROWS for k in ks])
        if not ks or n == 0:
            return
        starts = {k: sent[k] for k in ks}

        def body(i, carry):
            for k in ks:
                piece(k, pl.multiple_of(starts[k] + i * STEP_ROWS, 8), STEP_ROWS).start()
            return carry

        lax.fori_loop(0, n, body, 0)
        for k in ks:
            sent[k] += n * STEP_ROWS

    everyone = (1, 7, 2, 6, 3, 5, 4)

    def tell(stage):
        pl.semaphore_signal(known_lo.at[stage], inc=1, device_id=far_id(1), device_id_type=MESH)
        pl.semaphore_signal(
            known_hi.at[stage], inc=1, device_id=far_id(SECTIONS - 1), device_id_type=MESH
        )

    def hear(stage):
        pl.semaphore_wait(known_lo.at[stage], 1)
        pl.semaphore_wait(known_hi.at[stage], 1)

    tell(0)
    stream((1, 7), 8)
    for copy in loads[1:]:
        copy.start()
    hear(0)
    tell(1)
    stream((2, 6), 2)

    def far_copies(phase, src, dst):
        out = []
        for k in range(1, SECTIONS):
            out.append(
                pltpu.make_async_remote_copy(
                    src_ref=src(lax.rem(a + k, SECTIONS)),
                    dst_ref=dst,
                    send_sem=far_s.at[phase, k],
                    recv_sem=far_r.at[phase, SECTIONS - k],
                    device_id=far_id(k),
                    device_id_type=MESH,
                )
            )
        return out

    def loc_copies(phase, src, dst):
        out = []
        for m in range(1, NEAR):
            out.append(
                pltpu.make_async_remote_copy(
                    src_ref=src(lax.rem(c + m, NEAR)),
                    dst_ref=dst,
                    send_sem=loc_s.at[phase, m],
                    recv_sem=loc_r.at[phase, NEAR - m],
                    device_id=loc_id(m),
                    device_id_type=MESH,
                )
            )
        return out

    def duo_copies(phase, src, dst):
        return [
            pltpu.make_async_remote_copy(
                src_ref=src,
                dst_ref=dst,
                send_sem=duo_s.at[phase],
                recv_sem=duo_r.at[phase],
                device_id=duo_id,
                device_id_type=MESH,
            )
        ]

    def start(copies):
        for copy in copies:
            copy.start()

    def wait(copies):
        for copy in copies:
            copy.wait()

    block = nrm.shape[2]
    squares = jnp.zeros((seqs, 1), F32)
    for i in range(ROW_BLOCKS):
        x = hid[:, i * block : (i + 1) * block].astype(F32)
        squares = squares + jnp.sum(x * x, -1, keepdims=True)
    factor = lax.rsqrt(squares * (1.0 / width) + 1e-05)
    for i in range(ROW_BLOCKS):
        x = hid[:, i * block : (i + 1) * block].astype(F32)
        y = (x * factor * gain[:, i * block : (i + 1) * block]).astype(BF16)
        nrm[i] = y.astype(F32)

    hear(1)
    tell(2)
    stream((3, 5), 1)

    per_section = ROW_BLOCKS // SECTIONS
    mine = [nrm[order[per_section * a + i]].astype(BF16) for i in range(per_section)]
    normed = jnp.concatenate(mine, -1)
    loads[0].wait()
    units = w.shape[0] // HEAD_DIM
    half = units // 2
    for u in range(units):
        y = nt_dot(normed, w_v[u * HEAD_DIM : (u + 1) * HEAD_DIM, :])
        for b in range(seqs):
            p_tx[2 * b + u // half, u % half : u % half + 1, :] = y[b : b + 1, :]
    own_rows = pl.ds(pl.multiple_of(a * cols, 8), cols)
    keep = pltpu.make_async_copy(w_v.at[own_rows, :], recv.at[a], load_sem.at[4])
    keep.start()

    hear(2)
    copies = far_copies(0, lambda b: p_tx.at[b], p_rx.at[a])
    start(copies)
    stream(everyone, 1)
    p_rx[a] = p_tx[a]
    wait(copies)
    total = p_rx[0]
    for i in range(1, SECTIONS):
        total = total + p_rx[i]
    q_tx[...] = total.astype(BF16)
    q_all[s, c, a] = total.astype(BF16)

    copies = far_copies(1, lambda b: q_tx, q_all.at[s, c, a])
    start(copies)
    stream(everyone, 1)
    wait(copies)

    copies = loc_copies(0, lambda b: q_all.at[s, c], q_all.at[s, c])
    start(copies)
    stream(everyone, 1)
    wait(copies)

    copies = duo_copies(0, q_all.at[s], q_all.at[s])
    start(copies)
    wait(copies)

    rotated = HEADS + KV_HEADS
    for b in range(seqs):
        for j in range(2 * SECTIONS):
            rank = j // 2
            rows[b, j * half : (j + 1) * half, :] = q_all[rank % 2, rank // 2, 2 * b + j % 2][
                :half
            ].astype(F32)
        x = rows[b, :rotated, :]
        x = x * turn[b, 0:1, :] + pltpu.roll(x, 64, 1) * turn[b, 1:2, :]
        rows[b, :rotated, :] = x.astype(BF16).astype(F32)

    for copy in loads[1:3]:
        copy.wait()
    groups = HEADS // KV_HEADS
    inverse = 1.0 / math.sqrt(HEAD_DIM)
    pos_count = k_v.shape[1]
    first = (2 * t + s) * pos_count

    def one_sequence(b, carry):
        position = first + lax.broadcasted_iota(jnp.int32, (groups, pos_count), 1)
        usable = position < lengths[b]
        low = lax.broadcasted_iota(jnp.int32, (groups, HEAD_DIM), 1) < 64
        for k in range(KV_HEADS):
            lanes = slice(k * HEAD_DIM, (k + 1) * HEAD_DIM)
            q = rows[b, k * groups : (k + 1) * groups, :].astype(BF16)
            scores = nt_dot(q, k_v[b, :, lanes]) * inverse
            top = jnp.max(jnp.where(usable, scores, -1e30), -1, keepdims=True)
            weights = jnp.exp(jnp.where(usable, scores - top, -1e30))
            total = jnp.sum(weights, -1, keepdims=True)
            mix = jnp.dot(weights.astype(BF16), v_v[b, :, lanes], preferred_element_type=F32)
            stat = jnp.where(low, top, total)
            for g in range(groups):
                state[g % 2, g // 2, k, pl.ds(b, 1), :] = mix[g : g + 1, :]
                state[g % 2, g // 2, k, pl.ds(seqs + b, 1), :] = stat[g : g + 1, :]
        return carry

    lax.fori_loop(0, seqs, one_sequence, 0)

    def parted(ref):
        mix = ref[0:seqs, :]
        top, total = split_stat(ref[seqs : 2 * seqs, :])
        return mix, top, total

    def put(ref, part):
        mix, best, total = part
        ref[0:seqs, :] = mix
        ref[seqs : 2 * seqs, :] = joined_stat(best, total)

    copies = duo_copies(1, state.at[1 - s], a_rx1)
    start(copies)
    wait(copies)

    def merge_duo(i, carry):
        u, v = i // SECTIONS, i % SECTIONS
        put(a_tx.at[u, v], merged([parted(state.at[s, u, v]), parted(a_rx1.at[u, v])]))
        return carry

    lax.fori_loop(0, NEAR * SECTIONS, merge_duo, 0)

    copies = loc_copies(1, lambda m: a_tx.at[m], a_rx2.at[c])
    start(copies)
    stream(everyone, 1)
    a_rx2[c] = a_tx[c]
    wait(copies)

    def merge_loc(v, carry):
        put(state.at[0, 0, v], merged([parted(a_rx2.at[i, v]) for i in range(NEAR)]))
        return carry

    lax.fori_loop(0, SECTIONS, merge_loc, 0)

    copies = far_copies(2, lambda b: state.at[0, 0, b], a_rx3.at[a])
    start(copies)
    stream(everyone, 1)
    a_rx3[a] = state[0, 0, a]
    wait(copies)
    mix, best, total = merged([parted(a_rx3.at[i]) for i in range(SECTIONS)])

    head = groups * a + 2 * c + s

    def head_rows(at):
        return jnp.concatenate([rows[b, pl.ds(at, 1), :] for b in range(seqs)], 0)

    own_score = jnp.sum(head_rows(head) * head_rows(HEADS + a), -1, keepdims=True) * inverse
    highest = jnp.maximum(best, own_score)
    old_scale = jnp.exp(best - highest)
    own_weight = jnp.exp(own_score - highest)
    numerator = mix * old_scale + own_weight * head_rows(rotated + a)
    denominator = total * old_scale + own_weight
    attended = (numerator / denominator).astype(BF16)

    loads[3].wait()
    wide = 512
    for i in range(width // wide):
        y = jnp.dot(attended, wo_v[:, i * wide : (i + 1) * wide], preferred_element_type=F32)
        for j in range(wide // 128):
            part[i * (wide // 128) + j] = y[:, j * 128 : (j + 1) * 128]

    half_blocks = part.shape[0] // 2
    own_half = pl.ds(s * half_blocks, half_blocks)
    copies = duo_copies(2, part.at[pl.ds((1 - s) * half_blocks, half_blocks)], o_rx1)
    start(copies)
    wait(copies)
    part[own_half] = part[own_half] + o_rx1[...]

    def quarter(m):
        return part.at[pl.ds(s * half_blocks + m * SECTIONS, SECTIONS)]

    copies = loc_copies(2, quarter, o_rx2.at[c])
    start(copies)
    stream(everyone, 1)
    o_rx2[c] = part[pl.ds(s * half_blocks + c * SECTIONS, SECTIONS)]
    wait(copies)
    o_tx[...] = (o_rx2[0] + o_rx2[1]) + (o_rx2[2] + o_rx2[3])

    copies = far_copies(3, lambda b: o_tx.at[b], o_rx3.at[a])
    start(copies)
    stream(everyone, 1)
    o_rx3[a] = o_tx[a]
    wait(copies)
    total = o_rx3[0]
    for i in range(1, SECTIONS):
        total = total + o_rx3[i]
    col = pl.multiple_of((s * half_blocks + c * SECTIONS + a) * 128, 128)
    g_all[s, c, a] = (hid[:, pl.ds(col, 128)].astype(F32) + total).astype(BF16)

    copies = far_copies(4, lambda b: g_all.at[s, c, a], g_all.at[s, c, a])
    start(copies)
    stream(everyone, 1)
    wait(copies)

    copies = loc_copies(3, lambda m: g_all.at[s, c], g_all.at[s, c])
    start(copies)
    stream(everyone, 1)
    wait(copies)

    copies = duo_copies(3, g_all.at[s], g_all.at[s])
    start(copies)
    while any(sent[k] < cols for k in everyone):
        stream(everyone, 1)
    wait(copies)
    give = pltpu.make_async_copy(g_all, g_out, load_sem.at[5])
    give.start()
    keep.wait()
    give.wait()
    for k in everyone:
        piece(k, 0, cols).wait()


def place_kernel(order, recv, g_in, mixed, new, buf, in_sem, out_sem):
    block = buf.shape[2]
    per_section = ROW_BLOCKS // SECTIONS
    reads = []
    for i in range(ROW_BLOCKS):
        src = recv.at[i // per_section, :, pl.ds((i % per_section) * block, block)]
        copy = pltpu.make_async_copy(src, buf.at[i], in_sem.at[i])
        copy.start()
        reads.append(copy)
    blocks = g_in.shape[0] * g_in.shape[1] * g_in.shape[2]
    for j in range(blocks):
        mixed[:, j * 128 : (j + 1) * 128] = g_in[
            j // (NEAR * SECTIONS), (j // SECTIONS) % NEAR, j % SECTIONS
        ]
    writes = []
    for i in range(ROW_BLOCKS):
        reads[i].wait()
        at = pl.multiple_of(order[i] * block, 128)
        copy = pltpu.make_async_copy(buf.at[i], new.at[:, pl.ds(at, block)], out_sem.at[i])
        copy.start()
        writes.append(copy)
    for copy in writes:
        copy.wait()


def shards(hidden_in, norm_gain, wqkv_old, wo, key_cache, value_cache, lengths, section_order):
    seqs, width = hidden_in.shape
    _, _, rank_cols, rows_old = wqkv_old.shape
    cols = rank_cols // SECTIONS
    block = width // ROW_BLOCKS
    pos_count = key_cache.shape[1]

    half_dim = HEAD_DIM // 2
    freqs = 500000.0 ** (-jnp.arange(half_dim, dtype=F32) * 2.0 / HEAD_DIM)
    angles = lengths.astype(F32)[:, None] * freqs[None, :]
    cosine, sine = jnp.cos(angles), jnp.sin(angles)
    turn = jnp.stack(
        [jnp.concatenate([cosine, cosine], -1), jnp.concatenate([-sine, sine], -1)], 1
    )

    vmem = pl.BlockSpec(memory_space=pltpu.VMEM)
    smem = pl.BlockSpec(memory_space=pltpu.SMEM)
    hbm = pl.BlockSpec(memory_space=pl.ANY)
    dma = pltpu.SemaphoreType.DMA
    tile = (8, 128)
    recv, g_out = pl.pallas_call(
        main_kernel,
        name="stream_and_decode",
        out_shape=(
            jax.ShapeDtypeStruct((SECTIONS, cols, rows_old), BF16),
            jax.ShapeDtypeStruct((2, NEAR, SECTIONS, seqs, 128), BF16),
        ),
        in_specs=[vmem, vmem, vmem, smem, smem, hbm, hbm, hbm, hbm],
        out_specs=(hbm, hbm),
        scratch_shapes=[
            pltpu.VMEM((rank_cols, rows_old), BF16),
            pltpu.VMEM(wo.shape, BF16),
            pltpu.VMEM(key_cache.shape, BF16),
            pltpu.VMEM(value_cache.shape, BF16),
            pltpu.VMEM((ROW_BLOCKS, seqs, block), F32),
            pltpu.VMEM((SECTIONS, *tile), F32),
            pltpu.VMEM((SECTIONS, *tile), F32),
            pltpu.VMEM(tile, BF16),
            pltpu.VMEM((2, NEAR, SECTIONS, *tile), BF16),
            pltpu.VMEM((seqs, HEADS + 2 * KV_HEADS, HEAD_DIM), F32),
            pltpu.VMEM((2, NEAR, SECTIONS, *tile), F32),
            pltpu.VMEM((NEAR, SECTIONS, *tile), F32),
            pltpu.VMEM((NEAR, SECTIONS, *tile), F32),
            pltpu.VMEM((NEAR, SECTIONS, *tile), F32),
            pltpu.VMEM((SECTIONS, *tile), F32),
            pltpu.VMEM((width // 128, seqs, 128), F32),
            pltpu.VMEM((width // 256, seqs, 128), F32),
            pltpu.VMEM((NEAR, SECTIONS, seqs, 128), F32),
            pltpu.VMEM((SECTIONS, seqs, 128), F32),
            pltpu.VMEM((SECTIONS, seqs, 128), F32),
            pltpu.VMEM((2, NEAR, SECTIONS, seqs, 128), BF16),
            dma((6,)),
            dma((SECTIONS,)),
            dma((SECTIONS,)),
            dma((5, SECTIONS)),
            dma((5, SECTIONS)),
            dma((4, NEAR)),
            dma((4, NEAR)),
            dma((4,)),
            dma((4,)),
            pltpu.SemaphoreType.REGULAR((3,)),
            pltpu.SemaphoreType.REGULAR((3,)),
        ],
        compiler_params=pltpu.CompilerParams(collective_id=0, has_side_effects=True),
    )(
        hidden_in,
        norm_gain.reshape(1, width),
        turn,
        lengths,
        section_order,
        wqkv_old.reshape(rank_cols, rows_old),
        wo,
        key_cache,
        value_cache,
    )

    mixed_out, new_weight = pl.pallas_call(
        place_kernel,
        name="place",
        out_shape=(
            jax.ShapeDtypeStruct((seqs, width), BF16),
            jax.ShapeDtypeStruct((cols, width), BF16),
        ),
        in_specs=[smem, hbm, vmem],
        out_specs=(vmem, hbm),
        scratch_shapes=[
            pltpu.VMEM((ROW_BLOCKS, cols, block), BF16),
            dma((ROW_BLOCKS,)),
            dma((ROW_BLOCKS,)),
        ],
    )(section_order, recv, g_out)
    return mixed_out, new_weight[None, None]


def solution(mesh):
    placed = (
        P("replica", None),
        P("replica"),
        P(("replica", "tp"), "sub", None, None),
        P(("replica", "tp", "sub"), None),
        P("replica", ("tp", "sub"), None),
        P("replica", ("tp", "sub"), None),
        P("replica"),
        P("replica"),
    )
    return jax.shard_map(
        shards,
        mesh=mesh,
        in_specs=placed,
        out_specs=(P("replica", None), P(("replica", "tp"), "sub", None, None)),
        check_vma=False,
    )
```

time: 533 us -> 307 us (0.58)
  the two profiles are of different devices: /device:TPU:103 before, /device:TPU:108 now
where the time goes in v1:
time: 307 us; the launch traced here: 306 us
  Pallas kernels  304 us (99%)
    pallas_call x1, Pallas kernels, shards(): pl.pallas_call(main_kernel, name='stream_and_decode', out_shape=(jax.Shap...  300 us

profile of v1, /device:TPU:108, one launch (start us, length us, event | category | flops | bytes accessed | tf_op | source)
XLA Modules:
  0.0 306.3 jit_solution(7528115491569886531)
XLA Ops:
  0.6 0.7 convert_element_type.3
  1.3 0.1 multiply_cosine_fusion
  1.4 0.1 pad_maximum_fusion.1
  1.5 0.6 pad_maximum_fusion.turn
  2.1 299.9 %stream_and_decode.1 = (bf16[8,160,1024]{2,1,0:T(8,128)(2,1)}, bf16[2,4,8,4,128]{4,3,2,1,0:T(4,128)(2,1)}) custom-call(bf16[4,8192]{1,0:T(4,128)(2,1)} %hid.1, f32[1,8192]{1,0:T(1,128)} %bitcast.8, f32[4,2,128]{2,1,0:T(2,128)} %pad_maximum_fusion.turn, s32[4]{0:T(128)} %lengths.1, s32[16]{0:T(128)} %order.3, bf16[1280,1024]{1,0:T(8,128)(2,1)} %bitcast.7, ...), custom_call_target="tpu_custom_call" | custom-call | tf_op jit(solution)/shard_map/stream_and_decode/pallas_call | solution.py:435
  302.0 4.3 %place.1 = (bf16[4,8192]{1,0:T(4,128)(2,1)}, bf16[160,8192]{1,0:T(8,128)(2,1)}) custom-call(s32[16]{0:T(128)} %order.3, bf16[8,160,1024]{2,1,0:T(8,128)(2,1)} %get-tuple-element.6.recv, bf16[2,4,8,4,128]{4,3,2,1,0:T(4,128)(2,1)} %get-tuple-element.7.g_in), custom_call_target="tpu_custom_call" | custom-call | tf_op jit(solution)/shard_map/place/pallas_call | solution.py:491
  (1 shorter events, 0.0 us)
